TPU v7x, 64 devices: a 2x2x8 block of a 4x4x8 slice. The times are simulated.
64 devices in a mesh: rep: 8 (over x, y, core), dp: 8 (over z).
Axes of the slice: x: 2, y: 2, z: 8, core: 2. Of those that a mesh axis runs over, the one named last changes fastest.
The devices are a block of a 4x4x8 slice.
Arguments:
- x: bfloat16 [64, 4096, 512], P(('rep', 'dp')), parts along dimension 0
- dy: bfloat16 [64, 4096, 512], P(('rep', 'dp')), parts along dimension 0
- w_gate: bfloat16 [2, 512, 2048], replicated
- w_up: bfloat16 [2, 512, 2048], replicated
- w_down: bfloat16 [2, 2048, 512], replicated
- m_w_gate: float32 [2, 512, 2048], P(None, 'dp')
- m_w_up: float32 [2, 512, 2048], P(None, 'dp')
- m_w_down: float32 [2, 2048, 512], P(None, 'dp')
- v_w_gate: float32 [2, 512, 2048], P(None, 'dp')
- v_w_up: float32 [2, 512, 2048], P(None, 'dp')
- v_w_down: float32 [2, 2048, 512], P(None, 'dp')
Outputs:
- output 1: bfloat16 [16, 512, 2048], P('rep'), parts along dimension 0
- output 2: bfloat16 [16, 512, 2048], P('rep'), parts along dimension 0
- output 3: bfloat16 [16, 2048, 512], P('rep'), parts along dimension 0
- output 4: float32 [16, 512, 2048], P('rep', 'dp'), parts along dimension 0
- output 5: float32 [16, 512, 2048], P('rep', 'dp'), parts along dimension 0
- output 6: float32 [16, 2048, 512], P('rep', 'dp'), parts along dimension 0
- output 7: float32 [16, 512, 2048], P('rep', 'dp'), parts along dimension 0
- output 8: float32 [16, 512, 2048], P('rep', 'dp'), parts along dimension 0
- output 9: float32 [16, 2048, 512], P('rep', 'dp'), parts along dimension 0
There are 8 independent parts. A program takes and returns all parts, laid end to end along the dimension named above; an argument that names none is the same for every part.
All inputs are finite; a program needn't handle non-finite values.
Results may differ from a plain program's by a relative error of at most 0.02.
Values are sent between devices in bfloat16 or wider.
A program may use at most 768 MiB of HBM per device.

v0:
```python
import jax
import jax.numpy as jnp
from jax import lax

NAMES = ("w_gate", "w_up", "w_down")


def matmul(a, w):
    return jnp.dot(a, w, preferred_element_type=jnp.float32).astype(jnp.bfloat16)


def normed(h):
    wide = h.astype(jnp.float32)
    scale = lax.rsqrt(jnp.mean(wide**2, -1, keepdims=True) + 1e-6)
    return (wide * scale).astype(jnp.bfloat16)


def layer(h, w):
    a = normed(h)
    gate = jnp.dot(a, w["w_gate"], preferred_element_type=jnp.float32)
    up = jnp.dot(a, w["w_up"], preferred_element_type=jnp.float32)
    return h + matmul((jax.nn.silu(gate) * up).astype(jnp.bfloat16), w["w_down"])


def adamw(w, m, v, g):
    m = 0.9 * m + 0.1 * g
    v = 0.95 * v + 0.05 * g * g
    step = m * lax.rsqrt(v + 1e-8) + 0.1 * w
    return (w - 0.02 * step).astype(jnp.bfloat16), m, v


def stack(weights, h):
    for number in range(weights["w_gate"].shape[0]):
        h = layer(h, {name: w[number] for name, w in weights.items()})
    return h


def solution(mesh):
    groups = mesh.shape["rep"]

    def step(x, dy, *arrays):
        weights, m, v = (arrays[i : i + 3] for i in (0, 3, 6))
        x, dy = (t.reshape(groups, -1, *t.shape[1:]) for t in (x, dy))

        def of_a_group(x, dy):
            _, back = jax.vjp(lambda w: stack(w, x), dict(zip(NAMES, weights, strict=True)))
            by_weights = back(dy)[0]
            gradients = [by_weights[name].astype(jnp.float32) for name in NAMES]
            new = [adamw(w.astype(jnp.float32), m, v, g) for w, m, v, g in zip(weights, m, v, gradients, strict=True)]
            return tuple(one[which] for which in range(3) for one in new)

        return tuple(t.reshape(-1, *t.shape[2:]) for t in jax.vmap(of_a_group)(x, dy))

    return step
```

profile of v0, /device:TPU:28, one launch (start us, length us, event | category | flops | bytes accessed | tf_op | source)
XLA Modules:
  0.0 881.9 jit_solution(15269543990213983144)
XLA Ops:
  23.1 15.1 %convolution_convert_fusion.1 = bf16[4096,2048]{1,0:T(8,128)(2,1)} fusion(bf16[1,4096,512]{2,1,0:T(8,128)(2,1)} %param.17, bf16[2,2048,512]{2,1,0:T(8,128)(2,1)} %param.16), kind=kOutput, calls=%fused_computation.201 | convolution fusion | flops 8598323200 | bytes 23068672 | tf_op jit(solution)/vmap(transpose(jvp()))/dot_general | solution.py:9
  38.2 16.5 %fusion.215 = f32[4096,2048]{1,0:T(8,128)} fusion(bf16[2,512,2048]{2,1,0:T(8,128)(2,1)} %param.12, bf16[1,4096,512]{2,1,0:T(8,128)(2,1)S(1)} %copy-done.13, f32[4096]{0:T(1024)S(1)} %add_rsqrt_fusion), kind=kOutput, calls=%fused_computation.241 | convolution fusion | flops 8596226048 | bytes 39862272 | tf_op jit(solution)/vmap(jvp())/dot_general | solution.py:20
  54.7 31.5 %fusion.164 = (bf16[1,1,4096,2048]{3,2,1,0:T(8,128)(2,1)}, f32[4096,2048]{1,0:T(8,128)}) fusion(f32[4096,2048]{1,0:T(8,128)} %fusion.215, bf16[2,512,2048]{2,1,0:T(8,128)(2,1)} %param.15, bf16[1,4096,512]{2,1,0:T(8,128)(2,1)S(1)} %copy-done.13, f32[4096]{0:T(1024)S(1)} %add_rsqrt_fusion), kind=kOutput, calls=%fused_computation.191 | convolution fusion | flops 8646557696 | bytes 90193920 | tf_op jit(solution)/vmap(jvp())/dot_general | solution.py:21
  86.2 16.3 %fusion.174 = (f32[4096]{0:T(1024)S(1)}, bf16[1,1,4096,512]{2,3,1,0:T(8,128)(2,1)}) fusion(bf16[2,2048,512]{2,1,0:T(8,128)(2,1)} %param.16, bf16[1,1,4096,2048]{3,2,1,0:T(8,128)(2,1)} %get-tuple-element.263, bf16[1,4096,512]{1,2,0:T(8,128)(2,1)} %copy), kind=kOutput, calls=%fused_computation.213 | convolution fusion | flops 8600416256 | bytes 27279360 | tf_op jit(solution)/vmap(jvp())/dot_general | solution.py:9
  108.6 15.4 %fusion.203 = f32[4096,2048]{1,0:T(8,128)} fusion(bf16[1,1,4096,512]{2,3,1,0:T(8,128)(2,1)S(1)} %fusion.175, bf16[2,512,2048]{2,1,0:T(8,128)(2,1)S(1)} %copy-done.25), kind=kOutput, calls=%fused_computation.229 | convolution fusion | flops 8589934592 | bytes 39845888 | tf_op jit(solution)/vmap(jvp())/dot_general | solution.py:21
  124.1 44.6 %fusion.153 = (bf16[1,1,4096,2048]{3,2,1,0:T(8,128)(2,1)}, bf16[1,1,4096,2048]{3,2,1,0:T(8,128)(2,1)}, f32[4096,2048]{1,0:T(8,128)}) fusion(f32[4096,2048]{1,0:T(8,128)} %fusion.203, bf16[4096,2048]{1,0:T(8,128)(2,1)} %convolution_convert_fusion.1, bf16[2,512,2048]{2,1,0:T(8,128)(2,1)} %param.12, bf16[1,1,4096,512]{2,3,1,0:T(8,128)(2,1)} %copy-done.2), kind=kOutput, calls=%fused_computation.175 | convolution fusion | flops 8715763712 | bytes 123731968 | tf_op jit(solution)/vmap(jvp())/dot_general | solution.py:20
  168.7 27.6 %fusion.163 = bf16[1,1,4096,2048]{3,2,1,0:T(8,128)(2,1)} fusion(f32[4096,2048]{1,0:T(8,128)} %fusion.203, f32[4096,2048]{1,0:T(8,128)} %get-tuple-element.267), kind=kLoop, calls=%fused_computation.189 | loop fusion | flops 50331648 | bytes 83886080 | tf_op jit(solution)/vmap(jvp())/convert_element_type | solution.py:22
  196.3 21.3 %copy.2 = bf16[1,1,4096,2048]{2,3,1,0:T(8,128)(2,1)} copy(bf16[1,1,4096,2048]{3,2,1,0:T(8,128)(2,1)} %fusion.163) | data formatting | bytes 33554432
  224.1 63.8 %while.16 = (bf16[1,1,4096,2048]{2,3,1,0:T(8,128)(2,1)}, bf16[1,1,4096,512]{3,2,1,0:T(8,128)(2,1)}, f32[1,256,512]{2,1,0:T(8,128)S(1)}, f32[1,256,512]{2,1,0:T(8...) while((bf16[1,1,4096,2048]{2,3,1,0:T(8,128)(2,1)}, ...), condition=%wide.windowed_dot_general_cond_rs.4.clone, body=%wide.windowed_dot_general_body_rs.4.clone.sunk | while | flops 4312530944 | bytes 144704176 | solution.py:9
  249.4 8.8 collective-permute-done.18
  288.7 21.5 %copy.4 = bf16[1,1,4096,2048]{2,3,1,0:T(8,128)(2,1)} copy(bf16[1,1,4096,2048]{3,2,1,0:T(8,128)(2,1)} %get-tuple-element.263) | data formatting | bytes 33554432
  310.2 14.5 %fusion.180 = bf16[4096,512]{0,1:T(8,128)(2,1)} fusion(bf16[1,1,4096,2048]{3,2,1,0:T(8,128)(2,1)} %get-tuple-element.622, bf16[2,512,2048]{2,1,0:T(8,128)(2,1)} %param.15), kind=kOutput, calls=%fused_computation.218 | convolution fusion | flops 8589934592 | bytes 23068672 | tf_op jit(solution)/vmap(transpose(jvp()))/dot_general | solution.py:21
  324.8 18.0 %fusion.176 = (f32[4096]{0:T(1024)S(1)}, bf16[1,1,4096,512]{2,3,1,0:T(8,128)(2,1)}) fusion(bf16[1,1,4096,512]{2,3,1,0:T(8,128)(2,1)S(1)} %copy-done.14, bf16[4096,512]{0,1:T(8,128)(2,1)} %fusion.180, bf16[2,512,2048]{2,1,0:T(8,128)(2,1)} %param.12, bf16[1,1,4096,2048]{3,2,1,0:T(8,128)(2,1)} %get-tuple-element.544), kind=kOutput, calls=%fused_computation.215 | convolution fusion | flops 8600416256 | bytes 31473664 | tf_op jit(solution)/vmap(transpose(jvp()))/dot_general | solution.py:20
  355.0 52.5 %while.17 = (bf16[1,1,4096,2048]{2,3,1,0:T(8,128)(2,1)}, bf16[1,1,4096,512]{3,2,1,0:T(8,128)(2,1)}, f32[1,256,512]{2,1,0:T(8,128)S(1)}, f32[1,256,512]{2,1,0:T(8...) while((bf16[1,1,4096,2048]{2,3,1,0:T(8,128)(2,1)}, ...), condition=%wide.windowed_dot_general_cond_rs.5.clone, body=%wide.windowed_dot_general_body_rs.5.clone.sunk | while | flops 4312530944 | bytes 144704176 | solution.py:9
  409.5 71.6 %while.14 = (bf16[1,1,4096,512]{2,3,1,0:T(8,128)(2,1)}, bf16[1,1,4096,2048]{3,2,1,0:T(8,128)(2,1)}, f32[1,64,2048]{2,1,0:T(8,128)S(1)}, f32[1,64,2048]{2,1,0:T(8...) while((bf16[1,1,4096,512]{2,3,1,0:T(8,128)(2,1)}, ...), condition=%wide.windowed_dot_general_cond_rs.2.clone, body=%wide.windowed_dot_general_body_rs.2.clone.sunk | while | flops 4299948032 | bytes 60818020 | solution.py:21
  414.9 8.4 fusion.329
  453.0 8.4 fusion.329
  486.6 40.6 %convert_multiply_fusion = (bf16[1,1,4096,2048]{3,2,1,0:T(8,128)(2,1)}, bf16[1,1,4096,2048]{3,2,1,0:T(8,128)(2,1)}) fusion(f32[4096,2048]{1,0:T(8,128)} %fusion.215, f32[4096,2048]{1,0:T(8,128)} %get-tuple-element.264, bf16[2,2048,512]{2,1,0:T(8,128)(2,1)} %param.16, bf16[1,1,4096,512]{2,3,1,0:T(8,128)(2,1)} %fusion.198), kind=kOutput, calls=%fused_computation.170 | convolution fusion | flops 8724152320 | bytes 106954752 | tf_op jit(solution)/vmap(transpose(jvp()))/dot_general | solution.py:9
  527.3 72.8 %while.15 = (bf16[1,1,4096,512]{2,3,1,0:T(8,128)(2,1)}, bf16[1,1,4096,2048]{3,2,1,0:T(8,128)(2,1)}, f32[1,64,2048]{2,1,0:T(8,128)S(1)}, f32[1,64,2048]{2,1,0:T(8...) while((bf16[1,1,4096,512]{2,3,1,0:T(8,128)(2,1)}, ...), condition=%wide.windowed_dot_general_cond_rs.3.clone, body=%wide.windowed_dot_general_body_rs.3.clone.sunk | while | flops 4299948032 | bytes 62915200 | solution.py:21
  533.4 8.4 fusion.337
  570.1 8.4 fusion.337
  607.6 95.7 %while.12 = (bf16[1,1,4096,512]{2,3,1,0:T(8,128)(2,1)}, bf16[1,1,4096,2048]{3,2,1,0:T(8,128)(2,1)}, f32[1,64,2048]{2,1,0:T(8,128)S(1)}, f32[1,64,2048]{2,1,0:T(8...) while((bf16[1,1,4096,512]{2,3,1,0:T(8,128)(2,1)}, ...), condition=%wide.windowed_dot_general_cond_rs.clone, body=%wide.windowed_dot_general_body_rs.clone.sunk | while | flops 4299948032 | bytes 62915200 | solution.py:20
  640.9 13.6 %collective-permute-done.2 = f32[1,64,2048]{2,1,0:T(8,128)S(1)} collective-permute-done((f32[1,64,2048]{2,1,0:T(8,128)}, f32[1,64,2048]{2,1,0:T(8,128)S(1)}, u32[]{:S(2)}, u32[]{:S(2)}) %collective-permute-start.2) | collective-permute-done | bytes 524320 | tf_op jit(solution)/vmap(transpose(jvp()))/dot_general | solution.py:20
  664.5 8.4 fusion.313
  673.6 9.9 %collective-permute-done = f32[1,64,2048]{2,1,0:T(8,128)} collective-permute-done((f32[1,64,2048]{2,1,0:T(8,128)S(1)}, f32[1,64,2048]{2,1,0:T(8,128)}, u32[]{:S(2)}, u32[]{:S(2)}) %collective-permute-start) | collective-permute-done | bytes 524320 | tf_op jit(solution)/vmap(transpose(jvp()))/dot_general | solution.py:20
  709.3 91.9 %while.13 = (bf16[1,1,4096,512]{2,3,1,0:T(8,128)(2,1)}, bf16[1,1,4096,2048]{3,2,1,0:T(8,128)(2,1)}, f32[1,64,2048]{2,1,0:T(8,128)S(1)}, f32[1,64,2048]{2,1,0:T(8...) while((bf16[1,1,4096,512]{2,3,1,0:T(8,128)(2,1)}, ...), condition=%wide.windowed_dot_general_cond_rs.1.clone, body=%wide.windowed_dot_general_body_rs.1.clone.sunk | while | flops 4299948032 | bytes 60818020 | solution.py:20
  715.0 8.4 fusion.321
  743.5 13.6 %collective-permute-done.6 = f32[1,64,2048]{2,1,0:T(8,128)S(1)} collective-permute-done((f32[1,64,2048]{2,1,0:T(8,128)}, f32[1,64,2048]{2,1,0:T(8,128)S(1)}, u32[]{:S(2)}, u32[]{:S(2)}) %collective-permute-start.6) | collective-permute-done | bytes 524320 | tf_op jit(solution)/vmap(transpose(jvp()))/dot_general | solution.py:20
  765.7 8.4 fusion.321
  774.8 10.9 %collective-permute-done.4 = f32[1,64,2048]{2,1,0:T(8,128)} collective-permute-done((f32[1,64,2048]{2,1,0:T(8,128)S(1)}, f32[1,64,2048]{2,1,0:T(8,128)}, u32[]{:S(2)}, u32[]{:S(2)}) %collective-permute-start.4) | collective-permute-done | bytes 524320 | tf_op jit(solution)/vmap(transpose(jvp()))/dot_general | solution.py:20
  802.4 9.3 %collective-permute-done.25 = f32[1,64,2048]{2,1,0:T(8,128)S(1)} collective-permute-done((f32[1,64,2048]{2,1,0:T(8,128)}, f32[1,64,2048]{2,1,0:T(8,128)S(1)}, u32[]{:S(2)}, u32[]{:S(2)}) %collective-permute-start.25) | collective-permute-done | bytes 524320 | tf_op jit(solution)/vmap(transpose(jvp()))/dot_general | solution.py:20
  815.6 50.2 %all-gather.10.cloned.1.call-done = bf16[1,2,512,2048]{3,2,1,0:T(8,128)(2,1)} async-done(((bf16[1,2,64,2048]{3,2,1,0:T(8,128)(2,1)}), bf16[1,2,512,2048]{3,2,1,0:T(8,128)(2,1)}) %all-gather.10.cloned.1.call-update) | async-done | bytes 4194320 | tf_op jit(solution)/reshape | solution.py:52
  (290 shorter events, 383.5 us)
Async XLA Ops:
  7.2 808.4 %all-gather.14.cloned.1.call-start = ((), (), s32[]{:S(2)}) async-start(), calls=%async_computation.2 | async-start | bytes 4718592 | tf_op jit(solution)/reshape | solution.py:52
  224.1 19.4 %collective-permute-start.16 = (f32[1,256,512]{2,1,0:T(8,128)S(1)}, f32[1,256,512]{2,1,0:T(8,128)S(1)}, u32[]{:S(2)}, u32[]{:S(2)}) collective-permute-start(f32[1,256,512]{2,1,0:T(8,128)S(1)} %broadcast_select_fusion.32), channel_id=29, source_target_pairs={{0,1},{1,2},{2,3},{3,4},{4,5},{5,6},{6,7},{7,0},{8,9},{9,10},{10,1... | collective-permute-start | bytes 1572872 | tf_op jit(solution)/vmap(transpose(jvp()))/dot_general | solution.py:9
  226.4 17.1 %collective-permute-start.17 = (f32[1,256,512]{2,1,0:T(8,128)S(1)}, f32[1,256,512]{2,1,0:T(8,128)S(1)}, u32[]{:S(2)}, u32[]{:S(2)}) collective-permute-start(f32[1,256,512]{2,1,0:T(8,128)S(1)} %broadcast_select_fusion.33), channel_id=28, source_target_pairs={{0,7},{1,0},{2,1},{3,2},{4,3},{5,4},{6,5},{7,6},{8,15},{9,8},{10,9... | collective-permute-start | bytes 1572872 | tf_op jit(solution)/vmap(transpose(jvp()))/dot_general | solution.py:9
  287.9 313.5 %collective-permute-start.28 = (f32[1,256,512]{2,1,0:T(8,128)}, f32[1,256,512]{2,1,0:T(8,128)}, u32[]{:S(2)}, u32[]{:S(2)}) collective-permute-start(f32[1,256,512]{2,1,0:T(8,128)} %get-tuple-element.45), channel_id=32, source_target_pairs={{0,1},{1,2},{2,3},{3,4},{4,5},{5,6},{6,7},{7,0},{8,9},{9,10},{10,1... | collective-permute-start | bytes 1572872 | tf_op jit(solution)/vmap(transpose(jvp()))/dot_general | solution.py:9
  407.5 195.0 %collective-permute-start.29 = (f32[1,256,512]{2,1,0:T(8,128)}, f32[1,256,512]{2,1,0:T(8,128)}, u32[]{:S(2)}, u32[]{:S(2)}) collective-permute-start(f32[1,256,512]{2,1,0:T(8,128)} %get-tuple-element.47), channel_id=38, source_target_pairs={{0,1},{1,2},{2,3},{3,4},{4,5},{5,6},{6,7},{7,0},{8,9},{9,10},{10,1... | collective-permute-start | bytes 1572872 | tf_op jit(solution)/vmap(transpose(jvp()))/dot_general | solution.py:9
  409.6 20.2 %collective-permute-start.8 = (f32[1,64,2048]{2,1,0:T(8,128)S(1)}, f32[1,64,2048]{2,1,0:T(8,128)S(1)}, u32[]{:S(2)}, u32[]{:S(2)}) collective-permute-start(f32[1,64,2048]{2,1,0:T(8,128)S(1)} %broadcast_select_fusion.28), channel_id=16, source_target_pairs={{0,1},{1,2},{2,3},{3,4},{4,5},{5,6},{6,7},{7,0},{8,9},{9,10},{10,1... | collective-permute-start | bytes 1572872 | tf_op jit(solution)/vmap(transpose(jvp()))/dot_general | solution.py:21
  411.5 18.3 %collective-permute-start.9 = (f32[1,64,2048]{2,1,0:T(8,128)S(1)}, f32[1,64,2048]{2,1,0:T(8,128)S(1)}, u32[]{:S(2)}, u32[]{:S(2)}) collective-permute-start(f32[1,64,2048]{2,1,0:T(8,128)S(1)} %broadcast_select_fusion.29), channel_id=15, source_target_pairs={{0,7},{1,0},{2,1},{3,2},{4,3},{5,4},{6,5},{7,6},{8,15},{9,8},{10,9... | collective-permute-start | bytes 1572872 | tf_op jit(solution)/vmap(transpose(jvp()))/dot_general | solution.py:21
  447.7 15.7 %collective-permute-start.8 = (f32[1,64,2048]{2,1,0:T(8,128)S(1)}, f32[1,64,2048]{2,1,0:T(8,128)S(1)}, u32[]{:S(2)}, u32[]{:S(2)}) collective-permute-start(f32[1,64,2048]{2,1,0:T(8,128)S(1)} %broadcast_select_fusion.28), channel_id=16, source_target_pairs={{0,1},{1,2},{2,3},{3,4},{4,5},{5,6},{6,7},{7,0},{8,9},{9,10},{10,1... | collective-permute-start | bytes 1572872 | tf_op jit(solution)/vmap(transpose(jvp()))/dot_general | solution.py:21
  464.6 15.6 %collective-permute-start.10 = (f32[1,64,2048]{2,1,0:T(8,128)}, f32[1,64,2048]{2,1,0:T(8,128)S(1)}, u32[]{:S(2)}, u32[]{:S(2)}) collective-permute-start(f32[1,64,2048]{2,1,0:T(8,128)} %get-tuple-element.473), channel_id=18, source_target_pairs={{0,1},{1,2},{2,3},{3,4},{4,5},{5,6},{6,7},{7,0},{8,9},{9,10},{10,1... | collective-permute-start | bytes 1572872 | tf_op jit(solution)/vmap(transpose(jvp()))/dot_general | solution.py:21
  481.1 222.1 %collective-permute-start.26 = (f32[1,64,2048]{2,1,0:T(8,128)}, f32[1,64,2048]{2,1,0:T(8,128)}, u32[]{:S(2)}, u32[]{:S(2)}) collective-permute-start(f32[1,64,2048]{2,1,0:T(8,128)} %get-tuple-element.41), channel_id=19, source_target_pairs={{0,1},{1,2},{2,3},{3,4},{4,5},{5,6},{6,7},{7,0},{8,9},{9,10},{10,1... | collective-permute-start | bytes 1572872 | tf_op jit(solution)/vmap(transpose(jvp()))/dot_general | solution.py:21
  527.3 15.7 %collective-permute-start.12 = (f32[1,64,2048]{2,1,0:T(8,128)S(1)}, f32[1,64,2048]{2,1,0:T(8,128)}, u32[]{:S(2)}, u32[]{:S(2)}) collective-permute-start(f32[1,64,2048]{2,1,0:T(8,128)S(1)} %broadcast_select_fusion.30), channel_id=22, source_target_pairs={{0,1},{1,2},{2,3},{3,4},{4,5},{5,6},{6,7},{7,0},{8,9},{9,10},{10,1... | collective-permute-start | bytes 1572872 | tf_op jit(solution)/vmap(transpose(jvp()))/dot_general | solution.py:21
  545.0 15.1 %collective-permute-start.14 = (f32[1,64,2048]{2,1,0:T(8,128)}, f32[1,64,2048]{2,1,0:T(8,128)S(1)}, u32[]{:S(2)}, u32[]{:S(2)}) collective-permute-start(f32[1,64,2048]{2,1,0:T(8,128)} %get-tuple-element.482), channel_id=24, source_target_pairs={{0,1},{1,2},{2,3},{3,4},{4,5},{5,6},{6,7},{7,0},{8,9},{9,10},{10,1... | collective-permute-start | bytes 1572872 | tf_op jit(solution)/vmap(transpose(jvp()))/dot_general | solution.py:21
  564.0 15.2 %collective-permute-start.12 = (f32[1,64,2048]{2,1,0:T(8,128)S(1)}, f32[1,64,2048]{2,1,0:T(8,128)}, u32[]{:S(2)}, u32[]{:S(2)}) collective-permute-start(f32[1,64,2048]{2,1,0:T(8,128)S(1)} %broadcast_select_fusion.30), channel_id=22, source_target_pairs={{0,1},{1,2},{2,3},{3,4},{4,5},{5,6},{6,7},{7,0},{8,9},{9,10},{10,1... | collective-permute-start | bytes 1572872 | tf_op jit(solution)/vmap(transpose(jvp()))/dot_general | solution.py:21
  581.2 16.0 %collective-permute-start.14 = (f32[1,64,2048]{2,1,0:T(8,128)}, f32[1,64,2048]{2,1,0:T(8,128)S(1)}, u32[]{:S(2)}, u32[]{:S(2)}) collective-permute-start(f32[1,64,2048]{2,1,0:T(8,128)} %get-tuple-element.482), channel_id=24, source_target_pairs={{0,1},{1,2},{2,3},{3,4},{4,5},{5,6},{6,7},{7,0},{8,9},{9,10},{10,1... | collective-permute-start | bytes 1572872 | tf_op jit(solution)/vmap(transpose(jvp()))/dot_general | solution.py:21
  581.9 16.0 %collective-permute-start.15 = (f32[1,64,2048]{2,1,0:T(8,128)S(1)}, f32[1,64,2048]{2,1,0:T(8,128)}, u32[]{:S(2)}, u32[]{:S(2)}) collective-permute-start(f32[1,64,2048]{2,1,0:T(8,128)S(1)} %get-tuple-element.483), channel_id=23, source_target_pairs={{0,7},{1,0},{2,1},{3,2},{4,3},{5,4},{6,5},{7,6},{8,15},{9,8},{10,9... | collective-permute-start | bytes 1572872 | tf_op jit(solution)/vmap(transpose(jvp()))/dot_general | solution.py:21
  600.1 104.3 %collective-permute-start.27 = (f32[1,64,2048]{2,1,0:T(8,128)}, f32[1,64,2048]{2,1,0:T(8,128)}, u32[]{:S(2)}, u32[]{:S(2)}) collective-permute-start(f32[1,64,2048]{2,1,0:T(8,128)} %get-tuple-element.43), channel_id=25, source_target_pairs={{0,1},{1,2},{2,3},{3,4},{4,5},{5,6},{6,7},{7,0},{8,9},{9,10},{10,1... | collective-permute-start | bytes 1572872 | tf_op jit(solution)/vmap(transpose(jvp()))/dot_general | solution.py:21
  607.5 208.1 %all-gather.12.cloned.1.call-start = ((), (), s32[]{:S(2)}) async-start(), calls=%async_computation.1 | async-start | bytes 4718592 | tf_op jit(solution)/reshape | solution.py:52
  607.8 19.4 %collective-permute-start = (f32[1,64,2048]{2,1,0:T(8,128)S(1)}, f32[1,64,2048]{2,1,0:T(8,128)}, u32[]{:S(2)}, u32[]{:S(2)}) collective-permute-start(f32[1,64,2048]{2,1,0:T(8,128)S(1)} %broadcast_select_fusion.24), channel_id=3, source_target_pairs={{0,1},{1,2},{2,3},{3,4},{4,5},{5,6},{6,7},{7,0},{8,9},{9,10},{10,1... | collective-permute-start | bytes 1572872 | tf_op jit(solution)/vmap(transpose(jvp()))/dot_general | solution.py:20
  608.8 18.4 %collective-permute-start.1 = (f32[1,64,2048]{2,1,0:T(8,128)}, f32[1,64,2048]{2,1,0:T(8,128)S(1)}, u32[]{:S(2)}, u32[]{:S(2)}) collective-permute-start(f32[1,64,2048]{2,1,0:T(8,128)} %broadcast_select_fusion.25), channel_id=2, source_target_pairs={{0,7},{1,0},{2,1},{3,2},{4,3},{5,4},{6,5},{7,6},{8,15},{9,8},{10,9... | collective-permute-start | bytes 1572872 | tf_op jit(solution)/vmap(transpose(jvp()))/dot_general | solution.py:20
  629.2 25.3 %collective-permute-start.2 = (f32[1,64,2048]{2,1,0:T(8,128)}, f32[1,64,2048]{2,1,0:T(8,128)S(1)}, u32[]{:S(2)}, u32[]{:S(2)}) collective-permute-start(f32[1,64,2048]{2,1,0:T(8,128)} %get-tuple-element.455), channel_id=5, source_target_pairs={{0,1},{1,2},{2,3},{3,4},{4,5},{5,6},{6,7},{7,0},{8,9},{9,10},{10,1... | collective-permute-start | bytes 1572872 | tf_op jit(solution)/vmap(transpose(jvp()))/dot_general | solution.py:20
  629.2 26.1 %collective-permute-start.3 = (f32[1,64,2048]{2,1,0:T(8,128)S(1)}, f32[1,64,2048]{2,1,0:T(8,128)}, u32[]{:S(2)}, u32[]{:S(2)}) collective-permute-start(f32[1,64,2048]{2,1,0:T(8,128)S(1)} %get-tuple-element.456), channel_id=4, source_target_pairs={{0,7},{1,0},{2,1},{3,2},{4,3},{5,4},{6,5},{7,6},{8,15},{9,8},{10,9... | collective-permute-start | bytes 1572872 | tf_op jit(solution)/vmap(transpose(jvp()))/dot_general | solution.py:20
  658.4 25.0 %collective-permute-start = (f32[1,64,2048]{2,1,0:T(8,128)S(1)}, f32[1,64,2048]{2,1,0:T(8,128)}, u32[]{:S(2)}, u32[]{:S(2)}) collective-permute-start(f32[1,64,2048]{2,1,0:T(8,128)S(1)} %broadcast_select_fusion.24), channel_id=3, source_target_pairs={{0,1},{1,2},{2,3},{3,4},{4,5},{5,6},{6,7},{7,0},{8,9},{9,10},{10,1... | collective-permute-start | bytes 1572872 | tf_op jit(solution)/vmap(transpose(jvp()))/dot_general | solution.py:20
  659.4 24.1 %collective-permute-start.1 = (f32[1,64,2048]{2,1,0:T(8,128)}, f32[1,64,2048]{2,1,0:T(8,128)S(1)}, u32[]{:S(2)}, u32[]{:S(2)}) collective-permute-start(f32[1,64,2048]{2,1,0:T(8,128)} %broadcast_select_fusion.25), channel_id=2, source_target_pairs={{0,7},{1,0},{2,1},{3,2},{4,3},{5,4},{6,5},{7,6},{8,15},{9,8},{10,9... | collective-permute-start | bytes 1572872 | tf_op jit(solution)/vmap(transpose(jvp()))/dot_general | solution.py:20
  685.4 15.7 %collective-permute-start.3 = (f32[1,64,2048]{2,1,0:T(8,128)S(1)}, f32[1,64,2048]{2,1,0:T(8,128)}, u32[]{:S(2)}, u32[]{:S(2)}) collective-permute-start(f32[1,64,2048]{2,1,0:T(8,128)S(1)} %get-tuple-element.456), channel_id=4, source_target_pairs={{0,7},{1,0},{2,1},{3,2},{4,3},{5,4},{6,5},{7,6},{8,15},{9,8},{10,9... | collective-permute-start | bytes 1572872 | tf_op jit(solution)/vmap(transpose(jvp()))/dot_general | solution.py:20
  703.2 98.0 %collective-permute-start.24 = (f32[1,64,2048]{2,1,0:T(8,128)}, f32[1,64,2048]{2,1,0:T(8,128)}, u32[]{:S(2)}, u32[]{:S(2)}) collective-permute-start(f32[1,64,2048]{2,1,0:T(8,128)} %get-tuple-element.37), channel_id=6, source_target_pairs={{0,1},{1,2},{2,3},{3,4},{4,5},{5,6},{6,7},{7,0},{8,9},{9,10},{10,1... | collective-permute-start | bytes 1572872 | tf_op jit(solution)/vmap(transpose(jvp()))/dot_general | solution.py:20
  709.3 156.5 %all-gather.10.cloned.1.call-start = ((), (), s32[]{:S(2)}) async-start(), calls=%async_computation | async-start | bytes 4718592 | tf_op jit(solution)/reshape | solution.py:52
  709.7 20.2 %collective-permute-start.4 = (f32[1,64,2048]{2,1,0:T(8,128)S(1)}, f32[1,64,2048]{2,1,0:T(8,128)}, u32[]{:S(2)}, u32[]{:S(2)}) collective-permute-start(f32[1,64,2048]{2,1,0:T(8,128)S(1)} %broadcast_select_fusion.26), channel_id=9, source_target_pairs={{0,1},{1,2},{2,3},{3,4},{4,5},{5,6},{6,7},{7,0},{8,9},{9,10},{10,1... | collective-permute-start | bytes 1572872 | tf_op jit(solution)/vmap(transpose(jvp()))/dot_general | solution.py:20
  711.4 18.4 %collective-permute-start.5 = (f32[1,64,2048]{2,1,0:T(8,128)S(1)}, f32[1,64,2048]{2,1,0:T(8,128)S(1)}, u32[]{:S(2)}, u32[]{:S(2)}) collective-permute-start(f32[1,64,2048]{2,1,0:T(8,128)S(1)} %broadcast_select_fusion.27), channel_id=8, source_target_pairs={{0,7},{1,0},{2,1},{3,2},{4,3},{5,4},{6,5},{7,6},{8,15},{9,8},{10,9... | collective-permute-start | bytes 1572872 | tf_op jit(solution)/vmap(transpose(jvp()))/dot_general | solution.py:20
  731.8 25.3 %collective-permute-start.6 = (f32[1,64,2048]{2,1,0:T(8,128)}, f32[1,64,2048]{2,1,0:T(8,128)S(1)}, u32[]{:S(2)}, u32[]{:S(2)}) collective-permute-start(f32[1,64,2048]{2,1,0:T(8,128)} %get-tuple-element.464), channel_id=11, source_target_pairs={{0,1},{1,2},{2,3},{3,4},{4,5},{5,6},{6,7},{7,0},{8,9},{9,10},{10,1... | collective-permute-start | bytes 1572872 | tf_op jit(solution)/vmap(transpose(jvp()))/dot_general | solution.py:20
  733.1 24.1 %collective-permute-start.7 = (f32[1,64,2048]{2,1,0:T(8,128)S(1)}, f32[1,64,2048]{2,1,0:T(8,128)}, u32[]{:S(2)}, u32[]{:S(2)}) collective-permute-start(f32[1,64,2048]{2,1,0:T(8,128)S(1)} %get-tuple-element.465), channel_id=10, source_target_pairs={{0,7},{1,0},{2,1},{3,2},{4,3},{5,4},{6,5},{7,6},{8,15},{9,8},{10,9... | collective-permute-start | bytes 1572872 | tf_op jit(solution)/vmap(transpose(jvp()))/dot_general | solution.py:20
  760.3 25.3 %collective-permute-start.4 = (f32[1,64,2048]{2,1,0:T(8,128)S(1)}, f32[1,64,2048]{2,1,0:T(8,128)}, u32[]{:S(2)}, u32[]{:S(2)}) collective-permute-start(f32[1,64,2048]{2,1,0:T(8,128)S(1)} %broadcast_select_fusion.26), channel_id=9, source_target_pairs={{0,1},{1,2},{2,3},{3,4},{4,5},{5,6},{6,7},{7,0},{8,9},{9,10},{10,1... | collective-permute-start | bytes 1572872 | tf_op jit(solution)/vmap(transpose(jvp()))/dot_general | solution.py:20
  762.7 23.0 %collective-permute-start.5 = (f32[1,64,2048]{2,1,0:T(8,128)S(1)}, f32[1,64,2048]{2,1,0:T(8,128)S(1)}, u32[]{:S(2)}, u32[]{:S(2)}) collective-permute-start(f32[1,64,2048]{2,1,0:T(8,128)S(1)} %broadcast_select_fusion.27), channel_id=8, source_target_pairs={{0,7},{1,0},{2,1},{3,2},{4,3},{5,4},{6,5},{7,6},{8,15},{9,8},{10,9... | collective-permute-start | bytes 1572872 | tf_op jit(solution)/vmap(transpose(jvp()))/dot_general | solution.py:20
  (58 other events, 947.9 us)
Sparse Core Ops, SparseCore 0:
  607.6 76.8 all-gather.13
  709.4 79.6 all-gather.11
  815.6 50.0 all-gather.9
where the time goes:
time: 894 us; the launch traced here: 882 us
  matrix products  381 us (43%)
  waiting for transfers between devices  177 us (20%)
  other arithmetic  105 us (12%)
  local copies, waits for them, and re-layouts  91.1 us (10%)
  starting transfers between devices  88 us (10%)
  loops' own time  24.9 us (3%)
  between operations  15.1 us (2%)
    dot_general x11, matrix products, layer(): gate = jnp.dot(a, w['w_gate'], preferred_element_type=jnp.float32)  147 us
    dot_general x11, matrix products, layer(): up = jnp.dot(a, w['w_up'], preferred_element_type=jnp.float32)  129 us
    dot_general x11, matrix products, matmul(): jnp.dot(a, w, preferred_element_type=jnp.float32).astype(jnp.bfloat16)  105 us
    unnamed x51, local copies, waits for them, and re-layouts  80.2 us
    dot_general x18, waiting for transfers between devices, layer(): gate = jnp.dot(a, w['w_gate'], preferred_element_type=jnp.float32)  70.6 us
    reshape x3, waiting for transfers between devices, step(): t.reshape(-1, *t.shape[2:])  50.2 us
    dot_general x18, starting transfers between devices, matmul(): jnp.dot(a, w, preferred_element_type=jnp.float32).astype(jnp.bfloat16)  34.6 us
    dot_general x18, waiting for transfers between devices, matmul(): jnp.dot(a, w, preferred_element_type=jnp.float32).astype(jnp.bfloat16)  33.5 us
  transfers between devices with their start and end apart: 57, of which 29 were waited for; matrix products, arithmetic and copies ran while one was open for 39% of the time, Pallas kernels for 0%

commit v1 on v0

v1 whole, which is shorter than its diff:
```python
import functools

import jax
import jax.numpy as jnp
from jax import lax
from jax.experimental import pallas as pl
from jax.experimental.pallas import tpu as pltpu
from jax.sharding import PartitionSpec as P

F32, BF = jnp.float32, jnp.bfloat16
NT = (((1,), (1,)), ((), ()))
MESH = pl.DeviceIdType.MESH
VMEM_LIMIT = 66_000_000
WIDE = 512
NARROW = 256
TILE = 512
ANY = pl.BlockSpec(memory_space=pl.ANY)
VMEM = pl.BlockSpec(memory_space=pltpu.VMEM)


def dot(a, b):
    return jnp.dot(a, b, preferred_element_type=F32)


def dot_nt(a, b):
    return lax.dot_general(a, b, NT, preferred_element_type=F32)


def sigmoid(g):
    return 0.5 * jnp.tanh(0.5 * g) + 0.5


def norm_scale(wide):
    return lax.rsqrt(jnp.mean(wide * wide, -1, keepdims=True) + 1e-6)


def adamw(w, m, v, g):
    m = 0.9 * m + 0.1 * g
    v = 0.95 * v + 0.05 * g * g
    step = m * lax.rsqrt(v + 1e-8) + 0.1 * w
    return (w - 0.02 * step).astype(BF), m, v


def forward_kernel(x_ref, dy_ref, wg_ref, wu_ref, wd_ref, h_ref, a0_ref, a1_ref, a0t_ref, a1t_ref, dyt_ref):
    x = x_ref[...].astype(F32)
    a = (x * norm_scale(x)).astype(BF)
    a0_ref[...] = a
    a0t_ref[...] = a.T
    dyt_ref[...] = dy_ref[...].T
    acc = None
    for at in range(0, wg_ref.shape[1], WIDE):
        cols = slice(at, at + WIDE)
        g = dot(a, wg_ref[:, cols])
        u = dot(a, wu_ref[:, cols])
        part = dot((g * sigmoid(g) * u).astype(BF), wd_ref[cols, :])
        acc = part if acc is None else acc + part
    h = (x + acc.astype(BF).astype(F32)).astype(BF)
    h_ref[...] = h
    wide = h.astype(F32)
    a1 = (wide * norm_scale(wide)).astype(BF)
    a1_ref[...] = a1
    a1t_ref[...] = a1.T


def forward(x, dy, wg, wu, wd):
    tokens, dim = x.shape
    row = pl.BlockSpec((TILE, dim), lambda i: (i, 0))
    col = pl.BlockSpec((dim, TILE), lambda i: (0, i))
    first = lambda w: pl.BlockSpec((None, *w.shape[1:]), lambda i: (0, 0, 0))
    return pl.pallas_call(
        forward_kernel,
        grid=(tokens // TILE,),
        in_specs=[row, row, first(wg), first(wu), first(wd)],
        out_specs=[row] * 3 + [col] * 3,
        out_shape=[jax.ShapeDtypeStruct((tokens, dim), BF)] * 3 + [jax.ShapeDtypeStruct((dim, tokens), BF)] * 3,
        compiler_params=pltpu.CompilerParams(vmem_limit_bytes=VMEM_LIMIT),
        name="forward0",
    )(x, dy, wg, wu, wd)


def rest_kernel(
    n, h_hbm, a0_hbm, a1_hbm, a0t_hbm, a1t_hbm, dyt_hbm, dy_hbm, wg_hbm, wu_hbm, wd_hbm, mg_hbm, mu_hbm, md_hbm, vg_hbm, vu_hbm, vd_hbm,
    og_ref, ou_ref, od_ref, gg_out, gu_out, gd_out,
    a_ref, at_ref, d_ref, dt_ref, da_ref, act_ref, dg_ref, du_ref, sg_ref, su_ref, sd_ref, tg_ref, tu_ref, td_ref,
    rg_ref, ru_ref, rc_ref, rw_ref, mg_ref, mu_ref, md_ref, vg_ref, vu_ref, vd_ref, ng_ref, nu_ref, nd_ref,
    big_sem, stage_sem, moment_sem, row_sem, own_sem, ssem, rsem, dssem, drsem, gssem, grsem,
):
    me = lax.axis_index("dp")
    right, left = lax.rem(me + 1, n), lax.rem(me + n - 1, n)
    towards = (right, left)
    tokens, dim = a_ref.shape
    hidden = wg_hbm.shape[2]
    layers = wg_hbm.shape[0]
    share, dshare = dim // n, hidden // n
    piece = dshare // 2
    owners = WIDE // piece
    blocks = hidden // WIDE
    halves = blocks // 2
    tiles = tokens // TILE

    def remote(src, dst, send, recv, to):
        return pltpu.make_async_remote_copy(src_ref=src, dst_ref=dst, send_sem=send, recv_sem=recv, device_id={"dp": to}, device_id_type=MESH)

    barrier = pltpu.get_barrier_semaphore()
    for to in towards:
        pl.semaphore_signal(barrier, inc=1, device_id={"dp": to}, device_id_type=MESH)

    loads = [pltpu.make_async_copy(s, t, big_sem.at[i]) for i, (s, t) in enumerate(((a1_hbm, a_ref), (dy_hbm, d_ref), (a1t_hbm, at_ref), (dyt_hbm, dt_ref)))]

    def unit_start(block, e):
        return ((lax.rem(block, halves) * owners + e) * 2 + block // halves) * piece

    def stage(number):
        layer, block, slot = layers - 1 - number // blocks, lax.rem(number, blocks), lax.rem(number, 2)
        copies = []
        for e in range(owners):
            at = pl.multiple_of(unit_start(block, e), piece)
            here = pl.ds(e * piece, piece)
            copies.append(pltpu.make_async_copy(wg_hbm.at[layer, :, pl.ds(at, piece)], sg_ref.at[slot, :, here], stage_sem.at[slot, 0, e]))
            copies.append(pltpu.make_async_copy(wu_hbm.at[layer, :, pl.ds(at, piece)], su_ref.at[slot, :, here], stage_sem.at[slot, 1, e]))
            copies.append(pltpu.make_async_copy(wd_hbm.at[layer, pl.ds(at, piece), :], sd_ref.at[slot, here, :], stage_sem.at[slot, 2, e]))
        return copies

    for copy in stage(jnp.int32(0)):
        copy.start()
    for copy in loads:
        copy.start()
    moments = [
        pltpu.make_async_copy(s, t, moment_sem.at[i])
        for i, (s, t) in enumerate(((mg_hbm, mg_ref), (mu_hbm, mu_ref), (md_hbm, md_ref), (vg_hbm, vg_ref), (vu_hbm, vu_ref), (vd_hbm, vd_ref)))
    ]
    rows = [
        pltpu.make_async_copy(wg_hbm.at[:, pl.ds(pl.multiple_of(me * share, share), share), :], ng_ref, row_sem.at[0]),
        pltpu.make_async_copy(wu_hbm.at[:, pl.ds(pl.multiple_of(me * share, share), share), :], nu_ref, row_sem.at[1]),
        pltpu.make_async_copy(wd_hbm.at[:, pl.ds(pl.multiple_of(me * dshare, dshare), dshare), :], nd_ref, row_sem.at[2]),
    ]
    for copy in moments + rows:
        copy.start()

    def whose(c, k):
        return lax.rem(me + n - 1 - k + n, n) if c == 0 else lax.rem(me + 1 + k, n)

    def ring(k, term, slot, send, recv, finish):
        for c in range(2):
            to = towards[c]

            @pl.when(k == 0)
            def _():
                remote(term(c, whose(c, 0)), slot(c, 0), send(c), recv(c, 0), to).start()

            @pl.when(k > 0)
            def _():
                came = slot(c, k - 1)
                copy = remote(came, came, send(c), recv(c, k - 1), to)
                copy.wait_recv()
                copy.wait_send()
                total = (came[...].astype(F32) + term(c, whose(c, k))[...].astype(F32)).astype(BF)

                @pl.when(k < n - 1)
                def _():
                    came[...] = total
                    remote(came, slot(c, k), send(c), recv(c, k), to).start()

                @pl.when(k == n - 1)
                def _():
                    finish(c, total)

    def wide_ring(number, k):
        layer, block, slot = layers - 1 - number // blocks, lax.rem(number, blocks), lax.rem(number, 2)

        def finish(c, total):
            out = (gg_out, gu_out)[c]
            for e in range(owners):
                out[layer, :, pl.ds(pl.multiple_of(unit_start(block, e), piece), piece)] = total[:, e * piece : (e + 1) * piece]

        ring(
            k,
            lambda c, who: (tg_ref, tu_ref)[c].at[slot, pl.ds(pl.multiple_of(who * share, share), share), :],
            lambda c, hop: (rg_ref, ru_ref)[c].at[slot, hop],
            lambda c: ssem.at[c],
            lambda c, hop: rsem.at[c, slot, hop],
            finish,
        )

    def down_ring(number, k):
        layer, half = layers - 1 - number // 2, lax.rem(number, 2)
        part = piece // 2

        def finish(c, total):
            gd_out[layer, pl.ds(pl.multiple_of(half * piece + c * part, part), part), :] = total

        ring(
            k,
            lambda c, who: td_ref.at[half, pl.ds(pl.multiple_of(who * piece + c * part, part), part), :],
            lambda c, hop: (rc_ref, rw_ref)[c].at[half, hop],
            lambda c: dssem.at[c],
            lambda c, hop: drsem.at[c, half, hop],
            finish,
        )

    def update(layer):
        for g_ref, m_ref, v_ref, w_ref in ((gg_out, mg_ref, vg_ref, ng_ref), (gu_out, mu_ref, vu_ref, nu_ref), (gd_out, md_ref, vd_ref, nd_ref)):
            new, _, _ = adamw(w_ref[layer].astype(F32), m_ref[layer], v_ref[layer], g_ref[layer].astype(F32))
            w_ref[layer] = new

    def own(layer):
        return [
            pltpu.make_async_copy(ng_ref.at[layer], og_ref.at[layer, pl.ds(pl.multiple_of(me * share, share), share), :], own_sem.at[layer, 0]),
            pltpu.make_async_copy(nu_ref.at[layer], ou_ref.at[layer, pl.ds(pl.multiple_of(me * share, share), share), :], own_sem.at[layer, 1]),
            pltpu.make_async_copy(nd_ref.at[layer], od_ref.at[layer, pl.ds(pl.multiple_of(me * dshare, dshare), dshare), :], own_sem.at[layer, 2]),
        ]

    def gather(layer, k):
        for u in range(3):
            for c in range(2):
                part = share // 2 if u < 2 else dshare // 2
                if u < 2:
                    mine = (ng_ref, nu_ref)[c].at[layer, pl.ds(u * part, part), :]
                    place = lambda who: (og_ref, ou_ref)[c].at[layer, pl.ds(pl.multiple_of(who * share + u * part, part), part), :]
                else:
                    mine = nd_ref.at[layer, pl.ds(c * part, part), :]
                    place = lambda who: od_ref.at[layer, pl.ds(pl.multiple_of(who * dshare + c * part, part), part), :]
                at = lax.rem(me + n - k, n) if c == 0 else lax.rem(me + k, n)
                send, recv, to = gssem.at[c, u], grsem.at[layer, c, u], towards[c]

                @pl.when(k == 0)
                def _():
                    remote(mine, place(me), send, recv.at[0], to).start()

                @pl.when(k > 0)
                def _():
                    copy = remote(mine, place(at), send, recv.at[k - 1], to)
                    copy.wait_recv()
                    copy.wait_send()

                    @pl.when(k < n - 1)
                    def _():
                        remote(place(at), place(at), send, recv.at[k], to).start()

    def block(number, needs_da, tick):
        slot = lax.rem(number, 2)
        for copy in stage(number):
            copy.wait()

        @pl.when(number + 1 < layers * blocks)
        def _():
            for copy in stage(number + 1):
                copy.start()

        base = pl.multiple_of(lax.rem(lax.rem(number, blocks), halves) * owners * piece, WIDE)
        half = lax.rem(number, blocks) // halves
        for s in range(WIDE // NARROW):
            cols = slice(s * NARROW, (s + 1) * NARROW)

            def tile(t):
                here = pl.ds(pl.multiple_of(t * TILE, TILE), TILE)
                wg, wu, wd = sg_ref[slot, :, cols], su_ref[slot, :, cols], sd_ref[slot, cols, :]
                a, d = a_ref[here, :], d_ref[here, :]
                g, u = dot(a, wg), dot(a, wu)
                dact = dot_nt(d, wd).astype(BF).astype(F32)
                sig = sigmoid(g)
                silu = g * sig
                act_ref[here, :] = (silu * u).astype(BF)
                du = (dact * silu).astype(BF)
                dg = (dact * u * (sig + silu * (1.0 - sig))).astype(BF)
                du_ref[here, :] = du
                dg_ref[here, :] = dg
                if needs_da:
                    da_ref[here, :] += dot_nt(dg, wg) + dot_nt(du, wu)

            def two(i, carry):
                tile(2 * i)
                tile(2 * i + 1)
                tick(s * (tiles // 2) + i)
                return carry

            lax.fori_loop(0, tiles // 2, two, 0)
            if s == 0:

                @pl.when(number == 0)
                def _():
                    loads[2].wait()
                    loads[3].wait()

            tg_ref[slot, :, cols] = dot(at_ref[...], dg_ref[...]).astype(BF)
            tu_ref[slot, :, cols] = dot(at_ref[...], du_ref[...]).astype(BF)
            td_ref[half, pl.ds(base + s * NARROW, NARROW), :] = dot(dt_ref[...], act_ref[...]).T.astype(BF)

    def tick(number, point):
        @pl.when(number > 0)
        def _():
            wide_ring(number - 1, point)

        @pl.when(jnp.logical_and(number > 1, lax.rem(point, 2) == 1))
        def _():
            down_ring(number // 2 - 1, lax.rem(number, 2) * (n // 2) + point // 2)

    loads[0].wait()
    loads[1].wait()
    da_ref[...] = jnp.zeros_like(da_ref)
    pl.semaphore_wait(barrier, 2)

    def last_layer(number, carry):
        block(number, True, lambda point: tick(number, point))
        return carry

    lax.fori_loop(0, blocks, last_layer, 0)

    h_load = pltpu.make_async_copy(h_hbm, a_ref, big_sem.at[0])
    h_load.start()
    at_load = pltpu.make_async_copy(a0t_hbm, at_ref, big_sem.at[2])
    at_load.start()
    h_load.wait()

    def through_norm(t, carry):
        here = pl.ds(pl.multiple_of(t * TILE, TILE), TILE)
        h = a_ref[here, :].astype(F32)
        scale = norm_scale(h)
        da = da_ref[here, :].astype(BF).astype(F32)
        mean = jnp.mean(da * h, -1, keepdims=True)
        back = (scale * (da - h * (scale * scale * mean))).astype(BF).astype(F32)
        dh = (d_ref[here, :].astype(F32) + back).astype(BF)
        d_ref[here, :] = dh
        dt_ref[:, here] = dh.T
        return carry

    lax.fori_loop(0, tiles, through_norm, 0)
    a_load = pltpu.make_async_copy(a0_hbm, a_ref, big_sem.at[1])
    a_load.start()
    a_load.wait()
    at_load.wait()

    def first_layer(number, carry):
        block(number, False, lambda point: tick(number, point))
        return carry

    lax.fori_loop(blocks, blocks + halves, first_layer, 0)
    for copy in moments + rows:
        copy.wait()
    update(layers - 1)
    for copy in own(layers - 1):
        copy.start()
    lax.fori_loop(blocks + halves, 2 * blocks, first_layer, 0)

    def end(k, carry):
        wide_ring(2 * blocks - 1, k)
        down_ring(3, k)
        gather(layers - 1, k)
        return carry

    lax.fori_loop(0, n, end, 0)
    update(0)
    for copy in own(0):
        copy.start()

    def gather0(k, carry):
        gather(0, k)
        return carry

    lax.fori_loop(0, n, gather0, 0)
    for layer in range(layers):
        for copy in own(layer):
            copy.wait()


def rest(n, states, dy, w, m, v):
    tokens, dim = dy.shape
    layers, _, hidden = w[0].shape
    share, dshare = dim // n, hidden // n
    sds = jax.ShapeDtypeStruct
    dma = pltpu.SemaphoreType.DMA
    hops = n - 1
    return pl.pallas_call(
        functools.partial(rest_kernel, n),
        in_specs=[ANY] * 16,
        out_specs=[ANY] * 3 + [VMEM] * 3,
        out_shape=[sds(t.shape, BF) for t in w] + [sds(t.shape, BF) for t in m],
        scratch_shapes=[
            pltpu.VMEM((tokens, dim), BF),
            pltpu.VMEM((dim, tokens), BF),
            pltpu.VMEM((tokens, dim), BF),
            pltpu.VMEM((dim, tokens), BF),
            pltpu.VMEM((tokens, dim), F32),
            pltpu.VMEM((tokens, NARROW), BF),
            pltpu.VMEM((tokens, NARROW), BF),
            pltpu.VMEM((tokens, NARROW), BF),
            pltpu.VMEM((2, dim, WIDE), BF),
            pltpu.VMEM((2, dim, WIDE), BF),
            pltpu.VMEM((2, WIDE, dim), BF),
            pltpu.VMEM((2, dim, WIDE), BF),
            pltpu.VMEM((2, dim, WIDE), BF),
            pltpu.VMEM((2, hidden // 2, dim), BF),
            pltpu.VMEM((2, hops, share, WIDE), BF),
            pltpu.VMEM((2, hops, share, WIDE), BF),
            pltpu.VMEM((2, hops, dshare // 4, dim), BF),
            pltpu.VMEM((2, hops, dshare // 4, dim), BF),
            *[pltpu.VMEM(t.shape, F32) for t in (*m, *v)],
            *[pltpu.VMEM(t.shape, BF) for t in m],
            dma((4,)),
            dma((2, 3, WIDE // (dshare // 2))),
            dma((6,)),
            dma((3,)),
            dma((layers, 3)),
            dma((2,)),
            dma((2, 2, hops)),
            dma((2,)),
            dma((2, 2, hops)),
            dma((2, 3)),
            dma((layers, 2, 3, hops)),
        ],
        compiler_params=pltpu.CompilerParams(vmem_limit_bytes=VMEM_LIMIT, collective_id=0, has_side_effects=True),
        name="rest",
    )(*states, dy, *w, *m, *v)


def solution(mesh):
    n = mesh.shape["dp"]

    def step(x, dy, *arrays):
        w, m, v = (arrays[i : i + 3] for i in (0, 3, 6))
        x, dy = x[0], dy[0]
        states = forward(x, dy, *w)
        *new, gg, gu, gd = rest(n, states, dy, w, m, v)
        moments = [adamw(jnp.zeros((), F32), m, v, g.astype(F32))[1:] for m, v, g in zip(m, v, (gg, gu, gd), strict=True)]
        return (*new, *(one[0] for one in moments), *(one[1] for one in moments))

    seq, whole, block = P(("rep", "dp"), None, None), P(None, None, None), P(None, "dp", None)
    return jax.shard_map(
        step,
        mesh=mesh,
        in_specs=(seq, seq, *[whole] * 3, *[block] * 6),
        out_specs=(*[P("rep", None, None)] * 3, *[P("rep", "dp", None)] * 6),
        check_vma=False,
    )
```

time: 894 us -> 449 us (0.50); the launches traced: 882 us -> 449 us
  Pallas kernels: 0 us -> 431 us
  matrix products: 381 us -> 0 us
  waiting for transfers between devices: 177 us -> 0 us
  other arithmetic: 105 us -> 7.3 us
  starting transfers between devices: 88 us -> 0 us
  local copies, waits for them, and re-layouts: 91.1 us -> 9.45 us
  loops' own time: 24.9 us -> 0 us
  between operations: 15.1 us -> 0.72 us
    pallas_call x0 -> x2, Pallas kernels: none -> 431 us  [the longest x1 396 us: rest(): pl.pallas_call(functools.partial(rest_kernel, n), in_specs=[ANY] * 16, ou...]
    dot_general x33 -> x0, matrix products: 381 us -> none  [the longest x11 147 us: layer(): gate = jnp.dot(a, w['w_gate'], preferred_element_type=jnp.float32)]
    dot_general x54 -> x0, waiting for transfers between devices: 127 us -> none  [the longest x18 70.6 us: layer(): gate = jnp.dot(a, w['w_gate'], preferred_element_type=jnp.float32)]
    dot_general x54 -> x0, starting transfers between devices: 87.8 us -> none  [the longest x18 34.6 us: matmul(): jnp.dot(a, w, preferred_element_type=jnp.float32).astype(jnp.bfloat16)]
    unnamed x51 -> x19, local copies, waits for them, and re-layouts: 80.2 us -> 9.45 us
    reshape x3 -> x0, waiting for transfers between devices: 50.2 us -> none  [step(): t.reshape(-1, *t.shape[2:])]
    dot_general x48 -> x0, other arithmetic: 42.9 us -> none  [the longest x8 15.9 us: layer(): gate = jnp.dot(a, w['w_gate'], preferred_element_type=jnp.float32)]
    convert_element_type x3 -> x0, other arithmetic: 36.4 us -> none  [the longest x1 27.6 us: layer(): (jax.nn.silu(gate) * up).astype(jnp.bfloat16)]
  transfers between devices with their start and end apart: 57 -> 0, of which waited for: 29 -> 0; matrix products, arithmetic and copies ran while one was open for 39% -> 0% of each run, Pallas kernels for 0% -> 0%
where the time goes in v1:
time: 449 us
  Pallas kernels  431 us (96%)
  local copies, waits for them, and re-layouts  9.45 us (2%)
  other arithmetic  7.3 us (2%)
    pallas_call x1, Pallas kernels, rest(): pl.pallas_call(functools.partial(rest_kernel, n), in_specs=[ANY] * 16, ou...  396 us
    pallas_call x1, Pallas kernels, forward(): pl.pallas_call(forward_kernel, grid=(tokens // TILE,), in_specs=[row, row...  35.6 us
    unnamed x19, local copies, waits for them, and re-layouts  9.45 us

profile of v1, /device:TPU:28, one launch (start us, length us, event | category | flops | bytes accessed | tf_op | source)
XLA Modules:
  0.0 448.7 jit_solution(8250466926717032601)
XLA Ops:
  0.6 35.6 %forward0.1 = (bf16[4096,512]{1,0:T(8,128)(2,1)}, bf16[4096,512]{1,0:T(8,128)(2,1)}, bf16[4096,512]{1,0:T(8,128)(2,1)}, bf16[512,4096]{1,0:T(8,128)(2,1)}, bf16[...) custom-call(bf16[4096,512]{1,0:T(8,128)(2,1)} %bitcast.4, bf16[4096,512]{1,0:T(8,128)(2,1)} %bitcast.2, ...), custom_call_target="tpu_custom_call" | custom-call | tf_op jit(solution)/shard_map/forward0/pallas_call | solution.py:70
  36.3 395.6 %rest.1 = (bf16[2,512,2048]{2,1,0:T(8,128)(2,1)}, bf16[2,512,2048]{2,1,0:T(8,128)(2,1)}, bf16[2,2048,512]{2,1,0:T(8,128)(2,1)}, bf16[2,64,2048]{2,1,0:T(8,128)(2...) custom-call(bf16[4096,512]{1,0:T(8,128)(2,1)} %get-tuple-element.21.h_hbm, ...), custom_call_target="tpu_custom_call" | custom-call | tf_op jit(solution)/shard_map/rest/pallas_call | solution.py:373
  431.8 0.0 copy-start
  431.8 0.0 copy-start.1
  431.9 0.0 copy-start.2
  431.9 0.0 copy-start.3
  431.9 0.0 copy-start.7
  431.9 3.5 fusion.5
  435.4 0.0 copy-done
  435.4 0.0 copy-done.1
  435.4 0.0 copy-done.2
  435.4 0.0 copy-done.3
  435.4 0.0 copy-done.7
  435.5 0.0 copy-start.6
  435.5 3.8 fusion.3
  439.2 0.0 copy-done.6
  439.2 0.0 copy-start.5
  439.2 2.1 copy.23
  441.4 1.6 copy-done.5
  442.9 0.0 copy-start.4
  442.9 2.1 copy.24
  445.1 1.6 copy-done.4
  446.6 2.0 copy.25
Async XLA Ops:
  431.8 3.6 copy-start
  431.8 3.6 copy-start.1
  431.9 3.6 copy-start.2
  431.9 3.6 copy-start.3
  431.9 3.6 copy-start.7
  435.5 3.8 copy-start.6
  439.2 3.7 copy-start.5
  442.9 3.7 copy-start.4

commit v2 on v1

--- a/solution.py
+++ b/solution.py
@@ -14,6 +14,7 @@
 WIDE = 512
 NARROW = 256
 TILE = 512
+SLOTS = 4
 ANY = pl.BlockSpec(memory_space=pl.ANY)
 VMEM = pl.BlockSpec(memory_space=pltpu.VMEM)
 
@@ -141,6 +142,7 @@
         return lax.rem(me + n - 1 - k + n, n) if c == 0 else lax.rem(me + 1 + k, n)
 
     def ring(k, term, slot, send, recv, finish):
+        k = jnp.asarray(k, jnp.int32)
         for c in range(2):
             to = towards[c]
 
@@ -166,7 +168,7 @@
                     finish(c, total)
 
     def wide_ring(number, k):
-        layer, block, slot = layers - 1 - number // blocks, lax.rem(number, blocks), lax.rem(number, 2)
+        layer, block, slot = layers - 1 - number // blocks, lax.rem(number, blocks), lax.rem(number, SLOTS)
 
         def finish(c, total):
             out = (gg_out, gu_out)[c]
@@ -177,7 +179,7 @@
             k,
             lambda c, who: (tg_ref, tu_ref)[c].at[slot, pl.ds(pl.multiple_of(who * share, share), share), :],
             lambda c, hop: (rg_ref, ru_ref)[c].at[slot, hop],
-            lambda c: ssem.at[c],
+            lambda c: ssem.at[c, slot],
             lambda c, hop: rsem.at[c, slot, hop],
             finish,
         )
@@ -238,7 +240,7 @@
                         remote(place(at), place(at), send, recv.at[k], to).start()
 
     def block(number, needs_da, tick):
-        slot = lax.rem(number, 2)
+        slot, kept = lax.rem(number, 2), lax.rem(number, SLOTS)
         for copy in stage(number):
             copy.wait()
 
@@ -249,8 +251,8 @@
 
         base = pl.multiple_of(lax.rem(lax.rem(number, blocks), halves) * owners * piece, WIDE)
         half = lax.rem(number, blocks) // halves
-        for s in range(WIDE // NARROW):
-            cols = slice(s * NARROW, (s + 1) * NARROW)
+        def narrow(s, carry):
+            cols = pl.ds(pl.multiple_of(s * NARROW, NARROW), NARROW)
 
             def tile(t):
                 here = pl.ds(pl.multiple_of(t * TILE, TILE), TILE)
@@ -268,32 +270,56 @@
                 if needs_da:
                     da_ref[here, :] += dot_nt(dg, wg) + dot_nt(du, wu)
 
-            def two(i, carry):
-                tile(2 * i)
-                tile(2 * i + 1)
-                tick(s * (tiles // 2) + i)
+            def two(first, i, carry):
+                tile(first + 2 * i)
+                tile(first + 2 * i + 1)
                 return carry
 
-            lax.fori_loop(0, tiles // 2, two, 0)
-            if s == 0:
-
-                @pl.when(number == 0)
-                def _():
-                    loads[2].wait()
-                    loads[3].wait()
-
-            tg_ref[slot, :, cols] = dot(at_ref[...], dg_ref[...]).astype(BF)
-            tu_ref[slot, :, cols] = dot(at_ref[...], du_ref[...]).astype(BF)
-            td_ref[half, pl.ds(base + s * NARROW, NARROW), :] = dot(dt_ref[...], act_ref[...]).T.astype(BF)
-
-    def tick(number, point):
-        @pl.when(number > 0)
-        def _():
-            wide_ring(number - 1, point)
-
-        @pl.when(jnp.logical_and(number > 1, lax.rem(point, 2) == 1))
-        def _():
-            down_ring(number // 2 - 1, lax.rem(number, 2) * (n // 2) + point // 2)
+            def half_of_tiles(i, carry):
+                lax.fori_loop(0, tiles // 4, functools.partial(two, i * (tiles // 2)), 0)
+
+                @pl.when(i == 0)
+                def _():
+                    tick(True, 2 * s)
+
+                @pl.when(i == 1)
+                def _():
+                    tick(False, 2 * s)
+
+                return carry
+
+            lax.fori_loop(0, 2, half_of_tiles, 0)
+
+            @pl.when(jnp.logical_and(number == 0, s == 0))
+            def _():
+                loads[2].wait()
+                loads[3].wait()
+
+            tg_ref[kept, :, cols] = dot(at_ref[...], dg_ref[...]).astype(BF)
+            tu_ref[kept, :, cols] = dot(at_ref[...], du_ref[...]).astype(BF)
+            tick(True, 2 * s + 1)
+            td_ref[half, pl.ds(pl.multiple_of(base + s * NARROW, NARROW), NARROW), :] = dot(dt_ref[...], act_ref[...]).T.astype(BF)
+            tick(False, 2 * s + 1)
+            return carry
+
+        lax.fori_loop(0, WIDE // NARROW, narrow, 0)
+
+    def tick(number, wide, turn):
+        if wide:
+
+            @pl.when(number > 1)
+            def _():
+                wide_ring(number - 2, n // 2 + turn)
+
+            @pl.when(number > 0)
+            def _():
+                wide_ring(number - 1, turn)
+
+        else:
+
+            @pl.when(number > 1)
+            def _():
+                down_ring(number // 2 - 1, lax.rem(number, 2) * (n // 2) + turn)
 
     loads[0].wait()
     loads[1].wait()
@@ -301,7 +327,7 @@
     pl.semaphore_wait(barrier, 2)
 
     def last_layer(number, carry):
-        block(number, True, lambda point: tick(number, point))
+        block(number, True, functools.partial(tick, number))
         return carry
 
     lax.fori_loop(0, blocks, last_layer, 0)
@@ -331,7 +357,7 @@
     at_load.wait()
 
     def first_layer(number, carry):
-        block(number, False, lambda point: tick(number, point))
+        block(number, False, functools.partial(tick, number))
         return carry
 
     lax.fori_loop(blocks, blocks + halves, first_layer, 0)
@@ -343,8 +369,12 @@
     lax.fori_loop(blocks + halves, 2 * blocks, first_layer, 0)
 
     def end(k, carry):
-        wide_ring(2 * blocks - 1, k)
-        down_ring(3, k)
+        @pl.when(k < n // 2)
+        def _():
+            wide_ring(layers * blocks - 2, n // 2 + k)
+
+        wide_ring(layers * blocks - 1, k)
+        down_ring(2 * layers - 1, k)
         gather(layers - 1, k)
         return carry
 
@@ -387,11 +417,11 @@
             pltpu.VMEM((2, dim, WIDE), BF),
             pltpu.VMEM((2, dim, WIDE), BF),
             pltpu.VMEM((2, WIDE, dim), BF),
-            pltpu.VMEM((2, dim, WIDE), BF),
-            pltpu.VMEM((2, dim, WIDE), BF),
+            pltpu.VMEM((SLOTS, dim, WIDE), BF),
+            pltpu.VMEM((SLOTS, dim, WIDE), BF),
             pltpu.VMEM((2, hidden // 2, dim), BF),
-            pltpu.VMEM((2, hops, share, WIDE), BF),
-            pltpu.VMEM((2, hops, share, WIDE), BF),
+            pltpu.VMEM((SLOTS, hops, share, WIDE), BF),
+            pltpu.VMEM((SLOTS, hops, share, WIDE), BF),
             pltpu.VMEM((2, hops, dshare // 4, dim), BF),
             pltpu.VMEM((2, hops, dshare // 4, dim), BF),
             *[pltpu.VMEM(t.shape, F32) for t in (*m, *v)],
@@ -401,8 +431,8 @@
             dma((6,)),
             dma((3,)),
             dma((layers, 3)),
-            dma((2,)),
-            dma((2, 2, hops)),
+            dma((2, SLOTS)),
+            dma((2, SLOTS, hops)),
             dma((2,)),
             dma((2, 2, hops)),
             dma((2, 3)),

time: 449 us -> 418 us (0.931)
  Pallas kernels: 431 us -> 401 us
    pallas_call x1, Pallas kernels: 396 us -> 365 us  [rest(): pl.pallas_call(functools.partial(rest_kernel, n), in_specs=[ANY] * 16, ou...]
where the time goes in v2:
time: 418 us
  Pallas kernels  401 us (96%)
  local copies, waits for them, and re-layouts  9.45 us (2%)
  other arithmetic  7.3 us (2%)
    pallas_call x1, Pallas kernels, rest(): pl.pallas_call(functools.partial(rest_kernel, n), in_specs=[ANY] * 16, ou...  365 us
    pallas_call x1, Pallas kernels, forward(): pl.pallas_call(forward_kernel, grid=(tokens // TILE,), in_specs=[row, row...  35.6 us
    unnamed x19, local copies, waits for them, and re-layouts  9.45 us

profile of v2, /device:TPU:28, one launch (start us, length us, event | category | flops | bytes accessed | tf_op | source)
XLA Modules:
  0.0 418.2 jit_solution(9321591804604997521)
XLA Ops:
  0.6 35.6 %forward0.1 = (bf16[4096,512]{1,0:T(8,128)(2,1)}, bf16[4096,512]{1,0:T(8,128)(2,1)}, bf16[4096,512]{1,0:T(8,128)(2,1)}, bf16[512,4096]{1,0:T(8,128)(2,1)}, bf16[...) custom-call(bf16[4096,512]{1,0:T(8,128)(2,1)} %bitcast.4, bf16[4096,512]{1,0:T(8,128)(2,1)} %bitcast.2, ...), custom_call_target="tpu_custom_call" | custom-call | tf_op jit(solution)/shard_map/forward0/pallas_call | solution.py:71
  36.3 365.1 %rest.1 = (bf16[2,512,2048]{2,1,0:T(8,128)(2,1)}, bf16[2,512,2048]{2,1,0:T(8,128)(2,1)}, bf16[2,2048,512]{2,1,0:T(8,128)(2,1)}, bf16[2,64,2048]{2,1,0:T(8,128)(2...) custom-call(bf16[4096,512]{1,0:T(8,128)(2,1)} %get-tuple-element.21.h_hbm, ...), custom_call_target="tpu_custom_call" | custom-call | tf_op jit(solution)/shard_map/rest/pallas_call | solution.py:403
  401.3 0.0 copy-start
  401.3 0.0 copy-start.1
  401.4 0.0 copy-start.2
  401.4 0.0 copy-start.3
  401.4 0.0 copy-start.7
  401.4 3.5 fusion.5
  404.9 0.0 copy-done
  404.9 0.0 copy-done.1
  404.9 0.0 copy-done.2
  404.9 0.0 copy-done.3
  405.0 0.0 copy-done.7
  405.0 0.0 copy-start.6
  405.0 3.8 fusion.3
  408.7 0.0 copy-done.6
  408.7 0.0 copy-start.5
  408.7 2.1 copy.23
  410.9 1.6 copy-done.5
  412.4 0.0 copy-start.4
  412.4 2.1 copy.24
  414.6 1.6 copy-done.4
  416.1 2.0 copy.25
Async XLA Ops:
  401.3 3.6 copy-start
  401.3 3.6 copy-start.1
  401.4 3.6 copy-start.2
  401.4 3.6 copy-start.3
  401.4 3.6 copy-start.7
  405.0 3.8 copy-start.6
  408.7 3.7 copy-start.5
  412.4 3.7 copy-start.4
